TPU v7x, 32 devices: a whole 2x2x4 slice. The times are simulated.
32 devices in a mesh: robot: 8 (over z, x), sub: 4 (over y, core).
Axes of the slice: x: 2, y: 2, z: 4, core: 2. Of those that a mesh axis runs over, the one named last changes fastest.
Arguments:
- landmark_copies: float32 [8, 4, 3, 512], P('robot', 'sub'), may hold values from -6 to 6
- dual_copies: float32 [8, 4, 3, 512], P('robot', 'sub'), may hold values from -4 to 4
- visibility: int32 [8, 4, 512], P('robot', 'sub'), may hold values from 0 to 511
- block_counts: int32 [8, 4, 8], P('robot', 'sub'), may hold values from 1 to 64, as said below
- consensus_old: float32 [8, 4, 3, 512], P('robot', 'sub'), may hold values from -6 to 6
- poses: float32 [8, 4, 6, 1024], P('robot', 'sub'), may hold values from -6 to 6
- inverse_blocks: float32 [8, 4, 36, 1024], P('robot', 'sub'), may hold values from -1.8 to 1.8
- jacobians: float32 [8, 4, 18, 4096], P('robot', 'sub'), may hold values from -3 to 3
- measurements: float32 [8, 4, 3, 4096], P('robot', 'sub'), may hold values from -6 to 6
- obs_pose: int32 [8, 4, 4096], P('robot', 'sub'), may hold values from 0 to 1023
- obs_slot: int32 [8, 4, 4096], P('robot', 'sub'), may hold values from 0 to 511, as said below
- edge_to: int32 [8, 4, 1024], P('robot', 'sub'), may hold values from 0 to 4095
- edge_offset: float32 [8, 4, 6, 1024], P('robot', 'sub'), may hold values from -3 to 3
Outputs:
- refined_poses: float32 [8, 4, 6, 1024], P('robot', 'sub')
- consensus: float32 [8, 4, 3, 512], P('robot', 'sub')
- dual_new: float32 [8, 4, 3, 512], P('robot', 'sub')
- residual_norms: float32 [2], replicated
Inputs may be any that keep to these rules, and one draw needn't show every extreme that they name: block_counts[r,s,d] counts the live slots at the head of block d; for every sub index some robot receives full blocks from every robot, which robot varies with the draw. `obs_slot`: each observation names a live slot of its own device.
All inputs are finite; a program needn't handle non-finite values.
Results may differ from a plain program's by a relative error of at most 0.0001.
Values sent between devices are 32-bit elements; how exact they have to be, the bound alone decides.
No kernel may reach another device: no remote copies, remote signals or barrier semaphores. Data moves between devices by JAX's collectives and lax.ppermute only.
A program may use at most 64 MiB of HBM per device.

v0:
```python
import jax
import jax.numpy as jnp
from jax import lax
from jax.sharding import PartitionSpec as P

penalty = 2.0


def body(
    landmark_copies,
    dual_copies,
    visibility,
    block_counts,
    consensus_old,
    poses,
    inverse_blocks,
    jacobians,
    measurements,
    obs_pose,
    obs_slot,
    edge_to,
    edge_offset,
):
    copies = landmark_copies[0, 0]
    duals = dual_copies[0, 0]
    slot_ids = visibility[0]
    counts = block_counts[0, 0]
    old_estimate = consensus_old[0, 0]
    robots = lax.axis_size("robot")
    slot_count = copies.shape[1]
    block_size = slot_count // robots
    owned = old_estimate.shape[1]
    live_mask = (
        (jnp.arange(block_size)[None, :] < counts[:, None]).reshape(slot_count).astype(jnp.float32)
    )
    outgoing = jnp.concatenate([(copies + duals) * live_mask[None, :], live_mask[None, :]], axis=0)
    received, received_ids = (
        lax.all_to_all(outgoing, "robot", split_axis=1, concat_axis=1, tiled=True),
        lax.all_to_all(slot_ids, "robot", split_axis=1, concat_axis=1, tiled=True),
    )
    owner_ids = received_ids[0]
    totals = jax.vmap(lambda entries: jax.ops.segment_sum(entries, owner_ids, num_segments=owned))(
        received
    )
    consensus = (old_estimate + totals[:3]) / (1.0 + totals[3:4])
    returning = consensus[:, owner_ids]
    back = lax.all_to_all(returning, "robot", split_axis=1, concat_axis=1, tiled=True)
    differ = (copies - back) * live_mask[None, :]
    dual_new = duals + differ
    primal = jnp.sum(differ * differ)
    change = consensus - old_estimate
    dualsum = penalty * penalty * jnp.sum(totals[3:4] * change * change)
    primal_all, dual_all = lax.psum((primal, dualsum), ("robot", "sub"))
    landmark_total = owned * robots * lax.axis_size("sub")
    residual_norms = jnp.sqrt(jnp.stack([primal_all, dual_all]) / landmark_total)
    pose_block = poses[0, 0]
    pose_count = pose_block.shape[1]
    robot_all = lax.all_gather(pose_block, "sub", axis=1, tiled=True)
    pose_far = robot_all[:, edge_to[0, 0]]
    copies_at = copies[:, obs_slot[0, 0]]
    error = measurements[0, 0] - copies_at
    jac_rows = jacobians[0, 0].reshape(3, 6, error.shape[1])
    pull = jnp.sum(jac_rows * error[:, None, :], axis=0)
    pose_ids = obs_pose[0, 0]
    grad_obs = jax.vmap(
        lambda entries: jax.ops.segment_sum(entries, pose_ids, num_segments=pose_count)
    )(pull)
    grad = grad_obs + pose_far - pose_block - edge_offset[0, 0]
    inverse = inverse_blocks[0, 0].reshape(6, 6, pose_count)
    delta = jnp.sum(inverse * grad[None, :, :], axis=1)
    refined = pose_block + delta
    return (refined[None, None], consensus[None, None], dual_new[None, None], residual_norms)


def solution(mesh):
    return jax.shard_map(
        body,
        mesh=mesh,
        in_specs=(
            P("robot", "sub", None, None),
            P("robot", "sub", None, None),
            P("robot", "sub", None),
            P("robot", "sub", None),
            P("robot", "sub", None, None),
            P("robot", "sub", None, None),
            P("robot", "sub", None, None),
            P("robot", "sub", None, None),
            P("robot", "sub", None, None),
            P("robot", "sub", None),
            P("robot", "sub", None),
            P("robot", "sub", None),
            P("robot", "sub", None, None),
        ),
        out_specs=(
            P("robot", "sub", None, None),
            P("robot", "sub", None, None),
            P("robot", "sub", None, None),
            P(),
        ),
        check_vma=False,
    )
```

profile of v0, /device:TPU:0, one launch (start us, length us, event | category | flops | bytes accessed | tf_op | source)
XLA Modules:
  0.0 154.9 jit_solution(5562532823633209940)
XLA Ops:
  0.6 0.5 broadcast.115
  1.1 1.3 reduce.16
  2.5 0.7 all_to_all.22
  3.2 7.3 %all-to-all-start = ((s32[1,8,64]{2,0,1:T(1,128)}), s32[1,8,64]{2,0,1:T(1,128)S(1)}, u32[]{:S(2)}, u32[]{:S(2)}) async-start(s32[1,8,64]{2,0,1:T(1,128)} %all_to_all.22), calls=%async_computation | async-start | bytes 8192 | tf_op jit(solution)/shard_map/all_to_all | solution.py:39
  10.4 0.7 fusion.8
  11.2 0.7 fusion.9
  11.9 0.8 copy.53
  12.7 0.7 add_reduce_fusion.1
  13.5 0.1 add.79
  13.6 0.7 compare_select_fusion
  14.3 1.4 copy.52
  15.7 14.1 %gather_fusion.1 = f32[4096,3]{1,0:T(8,128)} fusion(f32[3,512]{0,1:T(8,128)S(1)} %bitcast.54, s32[4096]{0:T(1024)S(1)} %broadcast_clamp_fusion), kind=kCustom, calls=%fused_computation.1 | custom fusion | bytes 114688 | tf_op jit(solution)/shard_map/gather | solution.py:60
  29.8 3.2 %bitcast_subtract_fusion = f32[3,4096]{0,1:T(8,128)} fusion(f32[4096,3]{1,0:T(8,128)} %gather_fusion.1, f32[1,1,3,4096]{2,3,1,0:T(8,128)S(1)} %copy.52), kind=kLoop, calls=%fused_computation.5 | loop fusion | flops 12288 | bytes 147456 | tf_op jit(solution)/shard_map/sub | solution.py:61
  33.0 2.3 %copy.54 = f32[3,4096]{1,0:T(4,128)S(1)} copy(f32[3,4096]{0,1:T(8,128)} %bitcast_subtract_fusion) | data formatting | bytes 98304 | tf_op jit(solution)/shard_map/sub | solution.py:61
  35.2 0.7 reduce.1
  36.1 2.0 %copy.55 = f32[4096,6]{1,0:T(8,128)} copy(f32[4096,6]{0,1:T(8,128)S(1)} %bitcast.57) | data formatting | bytes 196608 | tf_op jit(solution)/shard_map/reduce_sum | solution.py:63
  38.1 0.2 copy.51
  38.3 15.8 %all-gather = f32[1,1,6,4096]{2,3,1,0:T(8,128)S(1)} all-gather(f32[1,1,6,1024]{2,3,1,0:T(8,128)S(1)} %copy.51), channel_id=2, replica_groups=mesh['robot'=8,'sub'=4] {'sub'}, dimensions={3}, use_global_device_ids=true | all-gather | bytes 122880 | tf_op jit(solution)/shard_map/all_gather | solution.py:58
  54.1 1.0 copy.57
  55.1 2.8 %gather_fusion = f32[1024,6]{1,0:T(8,128)S(1)} fusion(f32[6,4096]{0,1:T(8,128)S(1)} %bitcast.55, s32[1024]{0:T(1024)S(1)} %broadcast_clamp_fusion.1), kind=kCustom, calls=%fused_computation | custom fusion | bytes 53248 | tf_op jit(solution)/shard_map/gather | solution.py:59
  58.0 22.9 %scatter_fusion = f32[6,1024]{0,1:T(8,128)S(1)} fusion(f32[6,1024]{0,1:T(8,128)S(1)} %bitcast.53, s32[4096]{0:T(1024)S(1)} %bitcast.67, f32[4096,6]{1,0:T(8,128)} %copy.55), kind=kCustom, calls=%fused_computation.3 | custom fusion | flops 24576 | bytes 311296 | tf_op jit(solution)/shard_map/vmap()/scatter-add | solution.py:66
  81.0 0.2 copy.58
  81.2 0.4 reduce
  81.7 0.7 reshape.262
  82.4 0.1 copy.59
  82.6 6.0 %all-to-all-start.1 = ((f32[8,1,256]{2,1,0:T(1,128)}), f32[8,1,256]{2,1,0:T(1,128)S(1)}, u32[]{:S(2)}, u32[]{:S(2)}) async-start(f32[8,1,256]{2,1,0:T(1,128)} %reshape.262), calls=%async_computation.1 | async-start | bytes 16384 | tf_op jit(solution)/shard_map/all_to_all | solution.py:38
  88.7 0.7 reduce.17
  89.4 5.7 %all-to-all-done.1 = f32[8,1,256]{2,1,0:T(1,128)S(1)} async-done(((f32[8,1,256]{2,1,0:T(1,128)}), f32[8,1,256]{2,1,0:T(1,128)S(1)}, u32[]{:S(2)}, u32[]{:S(2)}) %all-to-all-start.1) | async-done | bytes 8224 | tf_op jit(solution)/shard_map/all_to_all | solution.py:38
  95.1 0.5 broadcast.117
  95.6 0.7 reduce.18
  96.4 0.1 reshape.226
  96.5 0.1 copy.62
  96.6 2.3 %scatter_custom_fusion.1 = f32[4,512]{0,1:T(8,128)S(1)} fusion(s32[512]{0:T(512)S(1)} %reshape.227, f32[512,4]{1,0:T(8,128)S(1)} %copy.62, f32[]{:T(128)} %constant.10.clone.1), kind=kCustom, calls=%fused_computation.21 | custom fusion | flops 2048 | bytes 8196 | tf_op jit(solution)/shard_map/vmap()/scatter-add | solution.py:42
  98.9 0.3 slice_reduce_fusion
  99.2 0.8 fusion
  100.0 1.0 gather_fusion.2
  101.1 0.1 copy.63
  101.2 0.7 reshape.264
  101.9 3.3 %all-to-all-start.2 = ((f32[8,1,192]{2,1,0:T(1,128)}), f32[8,1,192]{2,1,0:T(1,128)S(1)}, u32[]{:S(2)}, u32[]{:S(2)}) async-start(f32[8,1,192]{2,1,0:T(1,128)} %reshape.264), calls=%async_computation.2 | async-start | bytes 16384 | tf_op jit(solution)/shard_map/all_to_all | solution.py:47
  105.3 0.6 reshape_add_fusion
  106.0 0.7 copy.68
  107.3 4.4 %all-to-all-done.2 = f32[8,1,192]{2,1,0:T(1,128)S(1)} async-done(((f32[8,1,192]{2,1,0:T(1,128)}), f32[8,1,192]{2,1,0:T(1,128)S(1)}, u32[]{:S(2)}, u32[]{:S(2)}) %all-to-all-start.2) | async-done | bytes 6176 | tf_op jit(solution)/shard_map/all_to_all | solution.py:47
  111.7 0.7 reduce.19
  112.5 0.2 copy.67
  112.7 0.7 fusion.4
  113.5 0.6 copy.69
  114.1 38.9 %all-reduce = (f32[1]{0:T(128)}, f32[1]{0:T(128)}) all-reduce(f32[1]{0:T(128)} %bitcast.22, f32[1]{0:T(128)} %bitcast.21), channel_id=1, replica_groups=mesh['robot'=8,'sub'=4] {'robot','sub'}, use_global_device_ids=true, to_apply=%region_7.0 | all-reduce | flops 2 | bytes 16 | tf_op jit(solution)/shard_map/psum | solution.py:53
  153.0 1.9 %fusion.10 = f32[2]{0:T(128)} fusion(f32[1]{0:T(128)} %get-tuple-element.22, f32[1]{0:T(128)} %get-tuple-element.23), kind=kLoop, calls=%fused_computation.41 | loop fusion | flops 4 | bytes 16 | tf_op jit(solution)/shard_map/sqrt | solution.py:55
  (43 shorter events, 0.8 us)
Async XLA Ops:
  3.2 79.4 %all-to-all-start = ((s32[1,8,64]{2,0,1:T(1,128)}), s32[1,8,64]{2,0,1:T(1,128)S(1)}, u32[]{:S(2)}, u32[]{:S(2)}) async-start(s32[1,8,64]{2,0,1:T(1,128)} %all_to_all.22), calls=%async_computation | async-start | bytes 8192 | tf_op jit(solution)/shard_map/all_to_all | solution.py:39
  33.0 2.3 %copy-start.1 = (f32[1,1,18,4096]{3,1,2,0:T(1,128)S(1)}, f32[1,1,18,4096]{3,1,2,0:T(1,128)}, u32[]{:S(2)}) copy-start(f32[1,1,18,4096]{3,1,2,0:T(1,128)} %param.20) | copy-start | bytes 884740
  35.2 2.8 %copy-start.3 = (f32[1,1,6,1024]{3,1,2,0:T(1,128)S(1)}, f32[1,1,6,1024]{3,1,2,0:T(1,128)}, u32[]{:S(2)}) copy-start(f32[1,1,6,1024]{3,1,2,0:T(1,128)} %param.18) | copy-start | bytes 73732
  38.1 16.0 %copy-start.9 = (s32[1,1,1024]{2,1,0:T(1,128)S(1)}, s32[1,1,1024]{2,1,0:T(1,128)}, u32[]{:S(2)}) copy-start(s32[1,1,1024]{2,1,0:T(1,128)} %param.24) | copy-start | bytes 12292
  38.1 16.0 %copy-start.5 = (f32[1,1,6,1024]{3,1,2,0:T(1,128)S(1)}, f32[1,1,6,1024]{3,1,2,0:T(1,128)}, u32[]{:S(2)}) copy-start(f32[1,1,6,1024]{3,1,2,0:T(1,128)} %param.25) | copy-start | bytes 73732
  38.1 19.9 %copy-start.7 = (s32[1,1,4096]{2,1,0:T(1,128)S(1)}, s32[1,1,4096]{2,1,0:T(1,128)}, u32[]{:S(2)}) copy-start(s32[1,1,4096]{2,1,0:T(1,128)} %param.22) | copy-start | bytes 49156
  57.9 23.0 %copy-start = (f32[1,1,6,1024]{2,3,1,0:T(8,128)S(1)}, f32[1,1,6,1024]{2,3,1,0:T(8,128)}, u32[]{:S(2)}) copy-start(f32[1,1,6,1024]{2,3,1,0:T(8,128)} %copy.57) | copy-start | bytes 73732
  58.0 23.2 %copy-start.2 = (f32[1,1,36,1024]{3,1,2,0:T(1,128)S(1)}, f32[1,1,36,1024]{3,1,2,0:T(1,128)}, u32[]{:S(2)}) copy-start(f32[1,1,36,1024]{3,1,2,0:T(1,128)} %param.19) | copy-start | bytes 442372
  80.9 1.5 copy-start.8
  81.6 31.9 %copy-start.4 = (f32[1,1,3,512]{3,1,2,0:T(1,128)S(1)}, f32[1,1,3,512]{3,1,2,0:T(1,128)}, u32[]{:S(2)}) copy-start(f32[1,1,3,512]{3,1,2,0:T(1,128)} %param.13) | copy-start | bytes 18436
  81.6 31.9 %copy-start.6 = (f32[1,1,3,512]{3,1,2,0:T(1,128)S(1)}, f32[1,1,3,512]{3,1,2,0:T(1,128)}, u32[]{:S(2)}) copy-start(f32[1,1,3,512]{3,1,2,0:T(1,128)} %param.14) | copy-start | bytes 18436
  82.6 12.5 %all-to-all-start.1 = ((f32[8,1,256]{2,1,0:T(1,128)}), f32[8,1,256]{2,1,0:T(1,128)S(1)}, u32[]{:S(2)}, u32[]{:S(2)}) async-start(f32[8,1,256]{2,1,0:T(1,128)} %reshape.262), calls=%async_computation.1 | async-start | bytes 16384 | tf_op jit(solution)/shard_map/all_to_all | solution.py:38
  101.9 9.8 %all-to-all-start.2 = ((f32[8,1,192]{2,1,0:T(1,128)}), f32[8,1,192]{2,1,0:T(1,128)S(1)}, u32[]{:S(2)}, u32[]{:S(2)}) async-start(f32[8,1,192]{2,1,0:T(1,128)} %reshape.264), calls=%async_computation.2 | async-start | bytes 16384 | tf_op jit(solution)/shard_map/all_to_all | solution.py:47
where the time goes:
time: 156 us; the launch traced here: 155 us
  blocking collectives  54.7 us (35%)
  other arithmetic  40.4 us (26%)
  local copies, waits for them, and re-layouts  31.6 us (20%)
  starting transfers between devices  16.6 us (11%)
  waiting for transfers between devices  10.1 us (6%)
  between operations  1.6 us (1%)
    psum x1, blocking collectives, body(): primal_all, dual_all = lax.psum((primal, dualsum), ('robot', 'sub'))  38.9 us
    scatter-add x1, other arithmetic, body(): jax.ops.segment_sum(entries, pose_ids, num_segments=pose_count)  22.9 us
    all_gather x1, blocking collectives, body(): robot_all = lax.all_gather(pose_block, 'sub', axis=1, tiled=True)  15.8 us
    gather x1, local copies, waits for them, and re-layouts, body(): copies_at = copies[:, obs_slot[0, 0]]  14.1 us
    all_to_all x1, starting transfers between devices, body(): lax.all_to_all(slot_ids, 'robot', split_axis=1, concat_axis=1, tiled=True)  7.28 us
    unnamed x32, local copies, waits for them, and re-layouts  7.06 us
    all_to_all x1, starting transfers between devices, body(): lax.all_to_all(outgoing, 'robot', split_axis=1, concat_axis=1, tiled=True)  6.01 us
    all_to_all x1, waiting for transfers between devices, body(): lax.all_to_all(outgoing, 'robot', split_axis=1, concat_axis=1, tiled=True)  5.69 us
  transfers between devices with their start and end apart: 3, of which 2 were waited for; matrix products, arithmetic and copies ran while one was open for 38% of the time, Pallas kernels for 0%

commit v1 on v0

--- a/solution.py
+++ b/solution.py
@@ -2,6 +2,7 @@
 import jax.numpy as jnp
 from jax import lax
 from jax.sharding import PartitionSpec as P
+from jax.lax import all_gather
 
 penalty = 2.0
 
@@ -55,7 +56,8 @@
     residual_norms = jnp.sqrt(jnp.stack([primal_all, dual_all]) / landmark_total)
     pose_block = poses[0, 0]
     pose_count = pose_block.shape[1]
-    robot_all = lax.all_gather(pose_block, "sub", axis=1, tiled=True)
+    low = all_gather(pose_block, axis_name="sub")
+    robot_all = jnp.concatenate(low, axis=1)
     pose_far = robot_all[:, edge_to[0, 0]]
     copies_at = copies[:, obs_slot[0, 0]]
     error = measurements[0, 0] - copies_at

time: 156 us -> 147 us (0.942)
  blocking collectives: 54.7 us -> 44.6 us
    all_gather x1, blocking collectives: 15.8 us -> 5.52 us  [body(): low = all_gather(pose_block, axis_name='sub')]
  transfers between devices with their start and end apart: 3 -> 3, of which waited for: 2 -> 2; matrix products, arithmetic and copies ran while one was open for 38% -> 41% of each run, Pallas kernels for 0% -> 0%
where the time goes in v1:
time: 147 us; the launch traced here: 146 us
  blocking collectives  44.6 us (30%)
  other arithmetic  40.4 us (27%)
  local copies, waits for them, and re-layouts  33 us (22%)
  starting transfers between devices  16.6 us (11%)
  waiting for transfers between devices  10.1 us (7%)
  between operations  1.65 us (1%)
    psum x1, blocking collectives, body(): primal_all, dual_all = lax.psum((primal, dualsum), ('robot', 'sub'))  39 us
    scatter-add x1, other arithmetic, body(): jax.ops.segment_sum(entries, pose_ids, num_segments=pose_count)  22.9 us
    gather x1, local copies, waits for them, and re-layouts, body(): copies_at = copies[:, obs_slot[0, 0]]  14.1 us
    unnamed x32, local copies, waits for them, and re-layouts  7.8 us
    all_to_all x1, starting transfers between devices, body(): lax.all_to_all(slot_ids, 'robot', split_axis=1, concat_axis=1, tiled=True)  7.28 us
    all_to_all x1, starting transfers between devices, body(): lax.all_to_all(outgoing, 'robot', split_axis=1, concat_axis=1, tiled=True)  6.01 us
    all_to_all x1, waiting for transfers between devices, body(): lax.all_to_all(outgoing, 'robot', split_axis=1, concat_axis=1, tiled=True)  5.69 us
    all_gather x1, blocking collectives, body(): low = all_gather(pose_block, axis_name='sub')  5.52 us
  transfers between devices with their start and end apart: 3, of which 2 were waited for; matrix products, arithmetic and copies ran while one was open for 41% of the time, Pallas kernels for 0%

profile of v1, /device:TPU:0, one launch (start us, length us, event | category | flops | bytes accessed | tf_op | source)
XLA Modules:
  0.0 146.3 jit_solution(16189412156546832474)
XLA Ops:
  0.6 0.5 broadcast.115
  1.1 1.3 reduce.16
  2.5 0.7 all_to_all.22
  3.2 7.3 %all-to-all-start = ((s32[1,8,64]{2,0,1:T(1,128)}), s32[1,8,64]{2,0,1:T(1,128)S(1)}, u32[]{:S(2)}, u32[]{:S(2)}) async-start(s32[1,8,64]{2,0,1:T(1,128)} %all_to_all.22), calls=%async_computation | async-start | bytes 8192 | tf_op jit(solution)/shard_map/all_to_all | solution.py:40
  10.4 0.7 fusion.8
  11.2 0.7 fusion.9
  11.9 5.5 %all-gather = f32[4,1,6,1024]{3,1,2,0:T(1,128)S(1)} all-gather(f32[1,1,6,1024]{3,1,2,0:T(1,128)} %param.18), channel_id=2, replica_groups=mesh['robot'=8,'sub'=4] {'sub'}, dimensions={0}, use_global_device_ids=true | all-gather | bytes 122880 | tf_op jit(solution)/shard_map/all_gather | solution.py:59
  17.4 1.0 copy.59
  18.4 0.8 copy.56
  19.2 0.7 add_reduce_fusion.1
  20.0 0.7 compare_select_fusion
  20.8 1.4 copy.55
  22.2 14.1 %gather_fusion.1 = f32[4096,3]{1,0:T(8,128)} fusion(f32[3,512]{0,1:T(8,128)S(1)} %bitcast.59, s32[4096]{0:T(1024)S(1)} %broadcast_clamp_fusion), kind=kCustom, calls=%fused_computation.1 | custom fusion | bytes 114688 | tf_op jit(solution)/shard_map/gather | solution.py:62
  36.3 3.2 %bitcast_subtract_fusion = f32[3,4096]{0,1:T(8,128)} fusion(f32[4096,3]{1,0:T(8,128)} %gather_fusion.1, f32[1,1,3,4096]{2,3,1,0:T(8,128)S(1)} %copy.55), kind=kLoop, calls=%fused_computation.5 | loop fusion | flops 12288 | bytes 147456 | tf_op jit(solution)/shard_map/sub | solution.py:63
  39.5 2.3 %copy.57 = f32[3,4096]{1,0:T(4,128)S(1)} copy(f32[3,4096]{0,1:T(8,128)} %bitcast_subtract_fusion) | data formatting | bytes 98304 | tf_op jit(solution)/shard_map/sub | solution.py:63
  41.7 0.7 reduce.1
  42.6 2.0 %copy.58 = f32[4096,6]{1,0:T(8,128)} copy(f32[4096,6]{0,1:T(8,128)S(1)} %bitcast.62) | data formatting | bytes 196608 | tf_op jit(solution)/shard_map/reduce_sum | solution.py:65
  44.6 0.7 copy.54
  45.3 1.0 copy.60
  46.4 2.8 %gather_fusion = f32[1024,6]{1,0:T(8,128)S(1)} fusion(f32[6,4096]{0,1:T(8,128)S(1)} %bitcast.60, s32[1024]{0:T(1024)S(1)} %broadcast_clamp_fusion.1), kind=kCustom, calls=%fused_computation | custom fusion | bytes 53248 | tf_op jit(solution)/shard_map/gather | solution.py:61
  49.2 22.9 %scatter_fusion = f32[6,1024]{0,1:T(8,128)S(1)} fusion(f32[6,1024]{0,1:T(8,128)S(1)} %bitcast.58, s32[4096]{0:T(1024)S(1)} %bitcast.73, f32[4096,6]{1,0:T(8,128)} %copy.58), kind=kCustom, calls=%fused_computation.3 | custom fusion | flops 24576 | bytes 311296 | tf_op jit(solution)/shard_map/vmap()/scatter-add | solution.py:68
  72.2 0.2 copy.61
  72.4 0.4 reduce
  73.0 0.7 reshape.270
  73.7 0.1 copy.62
  73.8 6.0 %all-to-all-start.1 = ((f32[8,1,256]{2,1,0:T(1,128)}), f32[8,1,256]{2,1,0:T(1,128)S(1)}, u32[]{:S(2)}, u32[]{:S(2)}) async-start(f32[8,1,256]{2,1,0:T(1,128)} %reshape.270), calls=%async_computation.1 | async-start | bytes 16384 | tf_op jit(solution)/shard_map/all_to_all | solution.py:39
  79.9 0.7 reduce.17
  80.7 5.7 %all-to-all-done.1 = f32[8,1,256]{2,1,0:T(1,128)S(1)} async-done(((f32[8,1,256]{2,1,0:T(1,128)}), f32[8,1,256]{2,1,0:T(1,128)S(1)}, u32[]{:S(2)}, u32[]{:S(2)}) %all-to-all-start.1) | async-done | bytes 8224 | tf_op jit(solution)/shard_map/all_to_all | solution.py:39
  86.3 0.5 broadcast.117
  86.9 0.7 reduce.18
  87.6 0.1 reshape.234
  87.7 0.1 copy.65
  87.9 2.3 %scatter_custom_fusion.1 = f32[4,512]{0,1:T(8,128)S(1)} fusion(s32[512]{0:T(512)S(1)} %reshape.235, f32[512,4]{1,0:T(8,128)S(1)} %copy.65, f32[]{:T(128)} %constant.10.clone.1), kind=kCustom, calls=%fused_computation.21 | custom fusion | flops 2048 | bytes 8196 | tf_op jit(solution)/shard_map/vmap()/scatter-add | solution.py:43
  90.2 0.3 slice_reduce_fusion
  90.5 0.8 fusion
  91.3 1.0 gather_fusion.2
  92.3 0.1 copy.66
  92.5 0.7 reshape.272
  93.2 3.3 %all-to-all-start.2 = ((f32[8,1,192]{2,1,0:T(1,128)}), f32[8,1,192]{2,1,0:T(1,128)S(1)}, u32[]{:S(2)}, u32[]{:S(2)}) async-start(f32[8,1,192]{2,1,0:T(1,128)} %reshape.272), calls=%async_computation.2 | async-start | bytes 16384 | tf_op jit(solution)/shard_map/all_to_all | solution.py:48
  96.5 0.6 reshape_add_fusion
  97.2 0.7 copy.71
  98.6 4.4 %all-to-all-done.2 = f32[8,1,192]{2,1,0:T(1,128)S(1)} async-done(((f32[8,1,192]{2,1,0:T(1,128)}), f32[8,1,192]{2,1,0:T(1,128)S(1)}, u32[]{:S(2)}, u32[]{:S(2)}) %all-to-all-start.2) | async-done | bytes 6176 | tf_op jit(solution)/shard_map/all_to_all | solution.py:48
  103.0 0.7 reduce.19
  103.7 0.2 copy.70
  104.0 0.7 fusion.4
  104.7 0.6 copy.72
  105.3 39.0 %all-reduce = (f32[1]{0:T(128)}, f32[1]{0:T(128)}) all-reduce(f32[1]{0:T(128)} %bitcast.24, f32[1]{0:T(128)} %bitcast.23), channel_id=1, replica_groups=mesh['robot'=8,'sub'=4] {'robot','sub'}, use_global_device_ids=true, to_apply=%region_7.0 | all-reduce | flops 2 | bytes 16 | tf_op jit(solution)/shard_map/psum | solution.py:54
  144.4 1.9 %fusion.10 = f32[2]{0:T(128)} fusion(f32[1]{0:T(128)} %get-tuple-element.22, f32[1]{0:T(128)} %get-tuple-element.23), kind=kLoop, calls=%fused_computation.42 | loop fusion | flops 4 | bytes 16 | tf_op jit(solution)/shard_map/sqrt | solution.py:56
  (45 shorter events, 1.0 us)
Async XLA Ops:
  3.2 70.6 %all-to-all-start = ((s32[1,8,64]{2,0,1:T(1,128)}), s32[1,8,64]{2,0,1:T(1,128)S(1)}, u32[]{:S(2)}, u32[]{:S(2)}) async-start(s32[1,8,64]{2,0,1:T(1,128)} %all_to_all.22), calls=%async_computation | async-start | bytes 8192 | tf_op jit(solution)/shard_map/all_to_all | solution.py:40
  39.5 2.3 %copy-start.1 = (f32[1,1,18,4096]{3,1,2,0:T(1,128)S(1)}, f32[1,1,18,4096]{3,1,2,0:T(1,128)}, u32[]{:S(2)}) copy-start(f32[1,1,18,4096]{3,1,2,0:T(1,128)} %param.20) | copy-start | bytes 884740
  42.6 2.7 %copy-start.9 = (s32[1,1,1024]{2,1,0:T(1,128)S(1)}, s32[1,1,1024]{2,1,0:T(1,128)}, u32[]{:S(2)}) copy-start(s32[1,1,1024]{2,1,0:T(1,128)} %param.24) | copy-start | bytes 12292
  42.6 2.7 %copy-start.5 = (f32[1,1,6,1024]{3,1,2,0:T(1,128)S(1)}, f32[1,1,6,1024]{3,1,2,0:T(1,128)}, u32[]{:S(2)}) copy-start(f32[1,1,6,1024]{3,1,2,0:T(1,128)} %param.25) | copy-start | bytes 73732
  44.6 4.6 %copy-start.7 = (s32[1,1,4096]{2,1,0:T(1,128)S(1)}, s32[1,1,4096]{2,1,0:T(1,128)}, u32[]{:S(2)}) copy-start(s32[1,1,4096]{2,1,0:T(1,128)} %param.22) | copy-start | bytes 49156
  49.2 23.0 %copy-start = (f32[1,1,6,1024]{2,3,1,0:T(8,128)S(1)}, f32[1,1,6,1024]{2,3,1,0:T(8,128)}, u32[]{:S(2)}) copy-start(f32[1,1,6,1024]{2,3,1,0:T(8,128)} %copy.60) | copy-start | bytes 73732
  49.2 23.2 %copy-start.3 = (f32[1,1,36,1024]{3,1,2,0:T(1,128)S(1)}, f32[1,1,36,1024]{3,1,2,0:T(1,128)}, u32[]{:S(2)}) copy-start(f32[1,1,36,1024]{3,1,2,0:T(1,128)} %param.19) | copy-start | bytes 442372
  72.1 1.5 %copy-start.8 = (f32[1,1,3,512]{3,1,2,0:T(1,128)S(1)}, f32[1,1,3,512]{3,1,2,0:T(1,128)}, u32[]{:S(2)}) copy-start(f32[1,1,3,512]{3,1,2,0:T(1,128)} %param.17) | copy-start | bytes 18436
  72.2 24.3 %copy-start.2 = (f32[1,1,6,1024]{3,1,2,0:T(1,128)S(1)}, f32[1,1,6,1024]{3,1,2,0:T(1,128)}, u32[]{:S(2)}) copy-start(f32[1,1,6,1024]{3,1,2,0:T(1,128)} %param.18) | copy-start | bytes 73732
  72.8 31.9 %copy-start.4 = (f32[1,1,3,512]{3,1,2,0:T(1,128)S(1)}, f32[1,1,3,512]{3,1,2,0:T(1,128)}, u32[]{:S(2)}) copy-start(f32[1,1,3,512]{3,1,2,0:T(1,128)} %param.13) | copy-start | bytes 18436
  72.8 31.9 %copy-start.6 = (f32[1,1,3,512]{3,1,2,0:T(1,128)S(1)}, f32[1,1,3,512]{3,1,2,0:T(1,128)}, u32[]{:S(2)}) copy-start(f32[1,1,3,512]{3,1,2,0:T(1,128)} %param.14) | copy-start | bytes 18436
  73.8 12.5 %all-to-all-start.1 = ((f32[8,1,256]{2,1,0:T(1,128)}), f32[8,1,256]{2,1,0:T(1,128)S(1)}, u32[]{:S(2)}, u32[]{:S(2)}) async-start(f32[8,1,256]{2,1,0:T(1,128)} %reshape.270), calls=%async_computation.1 | async-start | bytes 16384 | tf_op jit(solution)/shard_map/all_to_all | solution.py:39
  93.2 9.8 %all-to-all-start.2 = ((f32[8,1,192]{2,1,0:T(1,128)}), f32[8,1,192]{2,1,0:T(1,128)S(1)}, u32[]{:S(2)}, u32[]{:S(2)}) async-start(f32[8,1,192]{2,1,0:T(1,128)} %reshape.272), calls=%async_computation.2 | async-start | bytes 16384 | tf_op jit(solution)/shard_map/all_to_all | solution.py:48
